TPU v7x, 256 devices: a whole 4x4x8 slice. The times are simulated.
256 devices in a mesh: row: 16 (over z_hi, y), col: 16 (over z_lo, x, core).
Axes of the slice: x: 4, y: 4, z: 8 (z_hi: 4, z_lo: 2; z = z_hi * 2 + z_lo), core: 2. Of those that a mesh axis runs over, the one named last changes fastest.
Arguments:
- tokens: bfloat16 [8192, 4096], P('row', 'col'), may hold values from -6 to 6
- norm_gain: bfloat16 [4096], P('col'), may hold values from 0.099609375 to 1.8984375
- gate_weight: bfloat16 [4096, 10240], P('row', 'col'), may hold values from -0.09375 to 0.09375
- linear_weight: bfloat16 [4096, 10240], P('row', 'col'), may hold values from -0.09375 to 0.09375
- output_weight: bfloat16 [10240, 4096], P('col', 'row'), may hold values from -0.078125 to 0.078125
Outputs:
- block_out: bfloat16 [8192, 4096], P('row', 'col')
All inputs are finite; a program needn't handle non-finite values.
Results may differ from a plain program's by a relative error of at most 0.0065.
Values may be sent and summed in bfloat16 or wider, within the bound.
A program may use at most 128 MiB of HBM per device.

v0:
```python
import jax
import jax.numpy as jnp
from jax import lax
from jax.sharding import PartitionSpec as P


def turned_gather(arrays, axis, dims):
    turned = [jnp.moveaxis(a, dim, 0) for a, dim in zip(arrays, dims)]
    widths = [t[0].size for t in turned]
    both = jnp.concatenate([t.reshape(-1, w) for t, w in zip(turned, widths)], axis=1)
    filled = lax.all_gather(both, axis, axis=0, tiled=True)
    parts = jnp.split(filled, [sum(widths[:k]) for k in range(1, len(widths))], axis=1)
    return tuple(
        (
            jnp.moveaxis(b.reshape(-1, *t.shape[1:]), 0, dim)
            for b, t, dim in zip(parts, turned, dims)
        )
    )


def side_by_side(arrays, axis, dim, along):
    both = jnp.concatenate(arrays, axis=along)
    filled, at, gathered = (lax.all_gather(both, axis, axis=dim, tiled=True), 0, [])
    for a in arrays:
        gathered.append(lax.slice_in_dim(filled, at, at + a.shape[along], axis=along))
        at += a.shape[along]
    return tuple(gathered)


def add_rows(left, piece):
    return jnp.dot(left, piece, preferred_element_type=jnp.float32)


def local(tokens, norm_gain, gate_weight, linear_weight, output_weight):
    whole, gain_all = turned_gather((tokens, norm_gain), "col", (1, 0))
    values = whole.astype(jnp.float32)
    meansq = jnp.mean(values * values, axis=-1, keepdims=True)
    normed = (values * lax.rsqrt(meansq + 1e-06) * gain_all.astype(jnp.float32)).astype(
        jnp.bfloat16
    )
    pieces = side_by_side((gate_weight, linear_weight), "row", 0, 1)
    gate = add_rows(normed, pieces[0])
    linear = add_rows(normed, pieces[1])
    hidden = (jax.nn.gelu(gate, approximate=True) * linear).astype(jnp.bfloat16)
    terms = jnp.dot(
        hidden,
        lax.all_gather(output_weight, "row", axis=1, tiled=True),
        preferred_element_type=jnp.float32,
    )
    return lax.psum_scatter(terms, "col", scatter_dimension=1, tiled=True).astype(jnp.bfloat16)


def solution(mesh):
    return jax.shard_map(
        local,
        mesh=mesh,
        in_specs=(P("row", "col"), P("col"), P("row", "col"), P("row", "col"), P("col", "row")),
        out_specs=P("row", "col"),
        check_vma=False,
    )
```

profile of v0, /device:TPU:8, one launch (start us, length us, event | category | flops | bytes accessed | tf_op | source)
XLA Modules:
  0.0 385.9 jit_solution(17165300564856851926)
XLA Ops:
  6.5 0.0 all-gather.4.cloned.1.call-start
  6.5 0.7 reshape.19
  7.2 1.7 pad_maximum_fusion.1
  8.9 0.0 all-gather.4.cloned.1.call-update
  8.9 0.0 all-gather.6.cloned.1.call-start
  8.9 2.0 pad_maximum_fusion
  10.9 0.0 all-gather.6.cloned.1.call-update
  10.9 0.0 all-gather.8.cloned.1.call-start
  11.0 0.7 all-gather.8.cloned.1.call-update
  11.7 0.0 reduce-scatter.2.cloned.1.call-start
  11.7 48.1 %all-gather.4.cloned.1.call-done = bf16[4096,513]{0,1:T(8,128)(2,1)} async-done(((bf16[256,513]{0,1:T(8,128)(2,1)}), bf16[4096,513]{0,1:T(8,128)(2,1)}) %all-gather.4.cloned.1.call-update) | async-done | bytes 4202512 | tf_op jit(solution)/shard_map/all_gather | solution.py:11
  59.8 0.0 slice-start
  59.8 3.1 fusion
  62.9 0.9 slice_convert_fusion
  63.8 128.5 %all-gather.6.cloned.1.call-done = bf16[4096,1280]{1,0:T(8,128)(2,1)} async-done(((bf16[256,1280]{1,0:T(8,128)(2,1)}), bf16[4096,1280]{1,0:T(8,128)(2,1)}) %all-gather.6.cloned.1.call-update) | async-done | bytes 10485776 | tf_op jit(solution)/shard_map/all_gather | solution.py:23
  192.3 0.0 slice-start.1
  192.3 0.0 copy-start
  192.3 7.1 %fusion.5 = f32[512,640]{1,0:T(8,128)S(1)} fusion(bf16[4096,1280]{1,0:T(8,128)(2,1)} %all-gather.6.cloned.1.call-done, f32[4096]{0:T(1024)S(1)} %bitcast.7, f32[512]{0:T(512)S(1)} %add_rsqrt_fusion, bf16[4096,513]{0,1:T(8,128)(2,1)} %all-gather.4.cloned.1.call-done), kind=kOutput, calls=%fused_computation.7 | convolution fusion | flops 2692743168 | bytes 10766336 | tf_op jit(solution)/shard_map/dot_general | solution.py:31
  199.3 0.0 slice-done
  199.3 0.0 slice-done.1
  199.3 0.9 copy-done
  200.2 3.7 fusion.10
  203.9 87.6 %all-gather.8.cloned.1.call-done = bf16[640,4096]{1,0:T(8,128)(2,1)} async-done(((bf16[640,256]{1,0:T(8,128)(2,1)}), bf16[640,4096]{1,0:T(8,128)(2,1)}) %all-gather.8.cloned.1.call-update) | async-done | bytes 5242896 | tf_op jit(solution)/shard_map/all_gather | solution.py:47
  291.5 8.2 %fusion.22 = f32[512,4096]{1,0:T(8,128)} fusion(bf16[512,640]{1,0:T(8,128)(2,1)S(1)} %fusion.10, bf16[640,4096]{1,0:T(8,128)(2,1)} %all-gather.8.cloned.1.call-done), kind=kOutput, calls=%fused_computation.23 | convolution fusion | flops 2684354560 | bytes 14286848 | tf_op jit(solution)/shard_map/dot_general | solution.py:45
  299.7 0.0 reduce-scatter.2.cloned.1.call-update
  299.7 77.9 %reduce-scatter.2.cloned.1.call-done = f32[512,256]{1,0:T(8,128)} async-done(((f32[512,4096]{1,0:T(8,128)}), f32[512,256]{1,0:T(8,128)}) %reduce-scatter.2.cloned.1.call-update) | async-done | bytes 524304 | tf_op jit(solution)/shard_map/reduce_scatter | solution.py:50
  377.6 1.8 convert_element_type.29
  (2 shorter events, 0.0 us)
Async XLA Ops:
  6.5 53.2 %all-gather.4.cloned.1.call-start = ((), (), s32[]{:S(2)}) async-start(), calls=%async_computation.1 | async-start | bytes 4526080 | tf_op jit(solution)/shard_map/all_gather | solution.py:11
  8.9 183.4 %all-gather.6.cloned.1.call-start = ((), (), s32[]{:S(2)}) async-start(), calls=%async_computation.2 | async-start | bytes 11141120 | tf_op jit(solution)/shard_map/all_gather | solution.py:23
  10.9 280.6 %all-gather.8.cloned.1.call-start = ((), (), s32[]{:S(2)}) async-start(), calls=%async_computation.3 | async-start | bytes 5570560 | tf_op jit(solution)/shard_map/all_gather | solution.py:47
  11.7 365.9 %reduce-scatter.2.cloned.1.call-start = ((), (), s32[]{:S(2)}) async-start(), calls=%async_computation.4 | async-start | bytes 8912896 | tf_op jit(solution)/shard_map/reduce_scatter | solution.py:50
  59.8 139.6 %slice-start = ((s8[4259840]{0:T(1024)(128)(4,1)}), s8[65536]{0:T(1024)(128)(4,1)S(1)}, s32[]{:S(2)}) async-start(s8[4259840]{0:T(1024)(128)(4,1)} %bitcast.4), calls=%async_computation.5 | async-start | bytes 131072
  192.3 7.1 %slice-start.1 = ((s8[4259840]{0:T(1024)(128)(4,1)}), s8[4194304]{0:T(1024)(128)(4,1)S(1)}, s32[]{:S(2)}) async-start(s8[4259840]{0:T(1024)(128)(4,1)} %bitcast.4), calls=%async_computation.6 | async-start | bytes 8388608
  192.3 8.0 %copy-start = (bf16[4096,1280]{1,0:T(8,128)(2,1)S(1)}, bf16[4096,1280]{1,0:T(8,128)(2,1)}, u32[]{:S(2)}) copy-start(bf16[4096,1280]{1,0:T(8,128)(2,1)} %all-gather.6.cloned.1.call-done) | copy-start | bytes 31457284
Sparse Core Ops, SparseCore 0:
  9.1 50.6 all-gather.3
  62.2 130.0 all-gather.5
  194.7 96.7 all-gather.7
  299.8 77.6 reduce-scatter.1
where the time goes:
time: 386 us
  waiting for transfers between devices  343 us (89%)
  matrix products  18.9 us (5%)
  between operations  13.2 us (3%)
  other arithmetic  9.37 us (2%)
    all_gather x1, waiting for transfers between devices, side_by_side(): lax.all_gather(both, axis, axis=dim, tiled=True)  128 us
    all_gather x1, waiting for transfers between devices, local(): lax.all_gather(output_weight, 'row', axis=1, tiled=True)  87.6 us
    reduce_scatter x1, waiting for transfers between devices, local(): lax.psum_scatter(terms, 'col', scatter_dimension=1, tiled=True)  77.9 us
    all_gather x1, waiting for transfers between devices, turned_gather(): filled = lax.all_gather(both, axis, axis=0, tiled=True)  48.1 us
    dot_general x2, matrix products, add_rows(): return jnp.dot(left, piece, preferred_element_type=jnp.float32)  10.7 us
    dot_general x1, matrix products, local(): jnp.dot(hidden, lax.all_gather(output_weight, 'row', axis=1, tiled=True),...  8.15 us
  transfers between devices with their start and end apart: 4, of which 4 were waited for; matrix products, arithmetic and copies ran while one was open for 4% of the time, Pallas kernels for 0%

commit v1 on v0

--- a/solution.py
+++ b/solution.py
@@ -8,7 +8,8 @@
     turned = [jnp.moveaxis(a, dim, 0) for a, dim in zip(arrays, dims)]
     widths = [t[0].size for t in turned]
     both = jnp.concatenate([t.reshape(-1, w) for t, w in zip(turned, widths)], axis=1)
-    filled = lax.all_gather(both, axis, axis=0, tiled=True)
+    sent = jnp.stack([both] * lax.axis_size(axis))
+    filled = jnp.concatenate(lax.all_to_all(sent, axis, 0, 0), axis=0)
     parts = jnp.split(filled, [sum(widths[:k]) for k in range(1, len(widths))], axis=1)
     return tuple(
         (

time: 386 us -> 365 us (0.946)
  waiting for transfers between devices: 343 us -> 310 us
  local copies, waits for them, and re-layouts: 1.55 us -> 11.3 us
  starting transfers between devices: 0.12 us -> 5.88 us
    all_to_all x0 -> x1, waiting for transfers between devices: none -> 127 us  [turned_gather(): filled = jnp.concatenate(lax.all_to_all(sent, axis, 0, 0), axis=0)]
    all_gather x1, waiting for transfers between devices: 128 us -> 26.4 us  [side_by_side(): lax.all_gather(both, axis, axis=dim, tiled=True)]
    all_gather x1 -> x0, waiting for transfers between devices: 48.1 us -> none  [turned_gather(): filled = lax.all_gather(both, axis, axis=0, tiled=True)]
    all_gather x1, waiting for transfers between devices: 87.6 us -> 78 us  [local(): lax.all_gather(output_weight, 'row', axis=1, tiled=True)]
    all_to_all x0 -> x1, starting transfers between devices: none -> 5.8 us  [turned_gather(): filled = jnp.concatenate(lax.all_to_all(sent, axis, 0, 0), axis=0)]
    unnamed x6 -> x8, local copies, waits for them, and re-layouts: 0.9 us -> 5.24 us
  transfers between devices with their start and end apart: 4 -> 4, of which waited for: 4 -> 4; matrix products, arithmetic and copies ran while one was open for 4% -> 6% of each run, Pallas kernels for 0% -> 0%
where the time goes in v1:
time: 365 us
  waiting for transfers between devices  310 us (85%)
  matrix products  18.7 us (5%)
  between operations  13.2 us (4%)
  local copies, waits for them, and re-layouts  11.3 us (3%)
  starting transfers between devices  5.88 us (2%)
  other arithmetic  5.61 us (2%)
    all_to_all x1, waiting for transfers between devices, turned_gather(): filled = jnp.concatenate(lax.all_to_all(sent, axis, 0, 0), axis=0)  127 us
    all_gather x1, waiting for transfers between devices, local(): lax.all_gather(output_weight, 'row', axis=1, tiled=True)  78 us
    reduce_scatter x1, waiting for transfers between devices, local(): lax.psum_scatter(terms, 'col', scatter_dimension=1, tiled=True)  77.9 us
    all_gather x1, waiting for transfers between devices, side_by_side(): lax.all_gather(both, axis, axis=dim, tiled=True)  26.4 us
    dot_general x2, matrix products, add_rows(): return jnp.dot(left, piece, preferred_element_type=jnp.float32)  10.7 us
    dot_general x1, matrix products, local(): jnp.dot(hidden, lax.all_gather(output_weight, 'row', axis=1, tiled=True),...  8.07 us
  transfers between devices with their start and end apart: 4, of which 4 were waited for; matrix products, arithmetic and copies ran while one was open for 6% of the time, Pallas kernels for 0%

profile of v1, /device:TPU:8, one launch (start us, length us, event | category | flops | bytes accessed | tf_op | source)
XLA Modules:
  0.0 364.7 jit_solution(15707432477719718268)
XLA Ops:
  6.5 0.0 all-gather.3.cloned.1.call-start
  6.5 2.0 pad_maximum_fusion
  8.5 0.0 all-gather.3.cloned.1.call-update
  8.5 0.7 reshape.24
  9.2 1.0 pad_maximum_fusion.1
  10.2 2.3 stack.2
  12.4 5.8 %all-to-all-start = ((bf16[16,256,513]{1,2,0:T(8,128)(2,1)}), bf16[16,256,513]{1,2,0:T(8,128)(2,1)}, u32[]{:S(2)}, u32[]{:S(2)}) async-start(bf16[16,256,513]{1,2,0:T(8,128)(2,1)} %stack.2), calls=%async_computation | async-start | bytes 8519680 | tf_op jit(solution)/shard_map/all_to_all | solution.py:12
  18.2 0.0 all-gather.5.cloned.1.call-start
  18.3 0.7 all-gather.5.cloned.1.call-update
  19.0 0.0 reduce-scatter.2.cloned.1.call-start
  19.0 127.0 %all-to-all-done = bf16[16,256,513]{1,2,0:T(8,128)(2,1)} async-done(((bf16[16,256,513]{1,2,0:T(8,128)(2,1)}), bf16[16,256,513]{1,2,0:T(8,128)(2,1)}, u32[]{:S(2)}, u32[]{:S(2)}) %all-to-all-start) | async-done | bytes 4202528 | tf_op jit(solution)/shard_map/all_to_all | solution.py:12
  146.0 3.1 copy.10
  149.1 0.3 pad.4
  149.4 3.0 copy.8
  152.4 0.0 copy-start
  152.4 0.9 fusion
  153.3 1.0 copy-done
  154.3 26.4 %all-gather.3.cloned.1.call-done = bf16[4096,1280]{1,0:T(8,128)(2,1)} async-done(((bf16[256,1280]{1,0:T(8,128)(2,1)}), bf16[4096,1280]{1,0:T(8,128)(2,1)}) %all-gather.3.cloned.1.call-update) | async-done | bytes 10485776 | tf_op jit(solution)/shard_map/all_gather | solution.py:24
  180.7 0.0 copy-start.1
  180.8 0.0 copy-start.2
  180.8 7.0 %fusion.5 = f32[512,640]{1,0:T(8,128)S(1)} fusion(bf16[4096,1280]{1,0:T(8,128)(2,1)} %all-gather.3.cloned.1.call-done, f32[4096]{0:T(1024)S(1)} %bitcast.18, f32[512]{0:T(512)S(1)} %add_rsqrt_fusion, bf16[4096,513]{0,1:T(8,128)(2,1)} %bitcast.14), kind=kOutput, calls=%fused_computation.7 | convolution fusion | flops 2692743168 | bytes 10766336 | tf_op jit(solution)/shard_map/dot_general | solution.py:32
  187.8 0.0 copy-done.1
  187.8 0.9 copy-done.2
  188.7 3.6 fusion.10
  192.4 78.0 %all-gather.5.cloned.1.call-done = bf16[640,4096]{1,0:T(8,128)(2,1)} async-done(((bf16[640,256]{1,0:T(8,128)(2,1)}), bf16[640,4096]{1,0:T(8,128)(2,1)}) %all-gather.5.cloned.1.call-update) | async-done | bytes 5242896 | tf_op jit(solution)/shard_map/all_gather | solution.py:48
  270.4 8.1 %fusion.22 = f32[512,4096]{1,0:T(8,128)} fusion(bf16[512,640]{1,0:T(8,128)(2,1)S(1)} %fusion.10, bf16[640,4096]{1,0:T(8,128)(2,1)} %all-gather.5.cloned.1.call-done), kind=kOutput, calls=%fused_computation.24 | convolution fusion | flops 2684354560 | bytes 14286848 | tf_op jit(solution)/shard_map/dot_general | solution.py:46
  278.5 0.0 reduce-scatter.2.cloned.1.call-update
  278.5 77.9 %reduce-scatter.2.cloned.1.call-done = f32[512,256]{1,0:T(8,128)} async-done(((f32[512,4096]{1,0:T(8,128)}), f32[512,256]{1,0:T(8,128)}) %reduce-scatter.2.cloned.1.call-update) | async-done | bytes 524304 | tf_op jit(solution)/shard_map/reduce_scatter | solution.py:51
  356.4 1.8 convert_element_type.29
  (2 shorter events, 0.0 us)
Async XLA Ops:
  6.5 174.2 %all-gather.3.cloned.1.call-start = ((), (), s32[]{:S(2)}) async-start(), calls=%async_computation.2 | async-start | bytes 11141120 | tf_op jit(solution)/shard_map/all_gather | solution.py:24
  12.4 133.6 %all-to-all-start = ((bf16[16,256,513]{1,2,0:T(8,128)(2,1)}), bf16[16,256,513]{1,2,0:T(8,128)(2,1)}, u32[]{:S(2)}, u32[]{:S(2)}) async-start(bf16[16,256,513]{1,2,0:T(8,128)(2,1)} %stack.2), calls=%async_computation | async-start | bytes 8519680 | tf_op jit(solution)/shard_map/all_to_all | solution.py:12
  18.2 252.2 %all-gather.5.cloned.1.call-start = ((), (), s32[]{:S(2)}) async-start(), calls=%async_computation.3 | async-start | bytes 5570560 | tf_op jit(solution)/shard_map/all_gather | solution.py:48
  19.0 337.4 %reduce-scatter.2.cloned.1.call-start = ((), (), s32[]{:S(2)}) async-start(), calls=%async_computation.4 | async-start | bytes 8912896 | tf_op jit(solution)/shard_map/reduce_scatter | solution.py:51
  152.4 2.0 copy-start
  180.7 7.1 %copy-start.1 = (bf16[65,8,16,256]{3,1,2,0:T(8,128)(2,1)S(1)}, bf16[65,8,16,256]{3,1,2,0:T(8,128)(2,1)}, u32[]{:S(2)}) copy-start(bf16[65,8,16,256]{3,1,2,0:T(8,128)(2,1)} %copy-done) | copy-start | bytes 12779524
  180.8 8.0 %copy-start.2 = (bf16[4096,1280]{1,0:T(8,128)(2,1)S(1)}, bf16[4096,1280]{1,0:T(8,128)(2,1)}, u32[]{:S(2)}) copy-start(bf16[4096,1280]{1,0:T(8,128)(2,1)} %all-gather.3.cloned.1.call-done) | copy-start | bytes 31457284
Sparse Core Ops, SparseCore 0:
  9.8 170.9 all-gather.2
  183.1 87.2 all-gather.4
  278.6 77.6 reduce-scatter.1
